TPU v7x, 32 devices: a whole 2x2x4 slice. The times are simulated.
32 devices in a mesh: row: 8 (over y, x, core), col: 4 (over z).
Axes of the slice: x: 2, y: 2, z: 4, core: 2. Of those that a mesh axis runs over, the one named last changes fastest.
Arguments:
- vectors: bfloat16 [32, 1024, 512], P('col', 'row'), may hold values from -6 to 6
- right_factors: bfloat16 [32, 32, 1024, 128], P('row', 'col'), may hold values from -0.1875 to 0.1875
- left_factors: bfloat16 [32, 32, 1024, 128], P('row', 'col'), may hold values from -0.125 to 0.125
- tile_ranks: int32 [32, 32], P('row', 'col'), may hold values from 16 to 128
- owner_map: int32 [32], replicated, may hold values from 0 to 31, as said below
Outputs:
- applied: bfloat16 [32, 1024, 512], P('row', 'col')
Inputs may be any that keep to these rules, and one draw needn't show every extreme that they name: owner_map is a permutation of 0 to 31; the 4 stored tile rows held by index i of row (stored rows i * 4 to i * 4 + 3) belong to 4 different indices of row of applied, i + c mod 8 for the same 4 offsets c at every i.
All inputs are finite; a program needn't handle non-finite values.
Results may differ from a plain program's by a relative error of at most 0.0066.
Values may be sent and summed in bfloat16 or wider, within the bound.
A program may use at most 128 MiB of HBM per device.

v0:
```python
import functools

import jax
import jax.numpy as jnp
from jax import lax
from jax.experimental import pallas as pl
from jax.experimental.pallas import tpu as pltpu
from jax.sharding import PartitionSpec as P

MESH = pl.DeviceIdType.MESH
LANES = 128
HALF_PARTS = 4
FULL_PARTS = 2
MID_PIECES = 2
LAST_PIECES = 4


def chip_steps(n_chip):
    relayed = n_chip == 4
    return [1, 2] if relayed else list(range(1, n_chip)), relayed


def kernel(n_row, n_col, n_chunk, owner_map, tile_ranks, vectors, right, left, out, *scratch):
    (raw, gathered, right_raw, right_t, left_v, coeffs, share_part, own_part, z_send, z_recv, final) = scratch[:11]
    a_send = scratch[11]
    n_land = n_chunk - 1 + LAST_PIECES
    a_recv = scratch[12 : 12 + n_land]
    (load_sem, fac_sem, ag_ssem, ag_rsem, rl_ssem, rl_rsem, fw_ssem, fw_rsem, z_ssem, z_rsem, a_ssem, a_rsem) = scratch[
        12 + n_land :
    ]
    held, tiles, block, rank_width = right_raw.shape
    depth = vectors.shape[1]
    width = raw.shape[2]
    half_depth = depth // 2
    half_block = block // 2
    half_held = held // 2
    quarter = out.shape[1]
    n_chip = n_row // 2
    direct, relayed = chip_steps(n_chip)
    last = n_chunk - 1
    n_step = n_chunk + 1
    me = lax.axis_index("row")
    z = lax.axis_index("col")
    chip, core = me // 2, me % 2
    partner = me + 1 - 2 * core

    def chunk_of(v):
        return max(v - 1, 0)

    def half_of(v):
        return v if v < 2 else None

    def parts_of(v):
        return HALF_PARTS if v < 2 else FULL_PARTS

    def slot_of(v, p):
        return v * HALF_PARTS + p if v < 2 else 2 * HALF_PARTS + (v - 2) * FULL_PARTS + p

    def items_of(v):
        return (half_of(v) * half_held, half_held) if v < 2 else (0, held)

    def pieces_of(v):
        if v < 2:
            return half_held
        return LAST_PIECES if v == n_step - 1 else MID_PIECES

    def chip_at(offset):
        bits = 0
        for bit in (1, 2, 4, 8, 16):
            if bit < n_chip:
                has = (chip // bit) % 2
                bits = bits + bit * (1 - has if offset & bit else has)
        return bits

    barrier = pltpu.get_barrier_semaphore()
    for d in range(1, n_row):
        pl.semaphore_signal(barrier, inc=1, device_id=((me + d) % n_row, z), device_id_type=MESH)

    @pl.when(z > 0)
    def _():
        pl.semaphore_signal(barrier, inc=1, device_id=(me, z - 1), device_id_type=MESH)

    @pl.when(z < n_col - 1)
    def _():
        pl.semaphore_signal(barrier, inc=1, device_id=(me, z + 1), device_id_type=MESH)

    first_load = pltpu.make_async_copy(vectors.at[:, :, pl.ds(0, width)], raw, load_sem.at[0])
    first_load.start()
    right_load = pltpu.make_async_copy(right, right_raw, fac_sem.at[0])
    right_load.start()

    def own_load(c, k):
        return pltpu.make_async_copy(
            vectors.at[:, pl.ds(k * half_depth, half_depth), pl.ds(c * width, width)],
            gathered.at[c, :, k, pl.ds(pl.multiple_of(me * half_depth, half_depth), half_depth), :],
            load_sem.at[2 * c + k],
        )

    for c in range(1, n_chunk):
        for k in range(2):
            own_load(c, k).start()
    left_load = pltpu.make_async_copy(left, left_v, fac_sem.at[1])
    left_load.start()

    def swapped(value):
        return jnp.concatenate([value[:, width // 2 :], value[:, : width // 2]], axis=1)

    low_lanes = lax.broadcasted_iota(jnp.int32, (1, width), 1) < width // 2

    first_load.wait()
    my_rows = pl.ds(pl.multiple_of(me * half_depth, half_depth), half_depth)
    for j in range(tiles):
        top = raw[j, :half_depth].astype(jnp.float32)
        bottom = raw[j, half_depth:].astype(jnp.float32)
        gathered[0, j, 0, my_rows, :] = jnp.where(low_lanes, top, swapped(bottom)).astype(jnp.bfloat16)
        gathered[0, j, 1, my_rows, :] = jnp.where(low_lanes, swapped(top), bottom).astype(jnp.bfloat16)

    both = jnp.where(z > 0, 1, 0) + jnp.where(z < n_col - 1, 1, 0)
    pl.semaphore_wait(barrier, n_row - 1 + both)

    def rows_of(v, first, count, index):
        rows = pl.ds(pl.multiple_of(index * half_depth, half_depth), half_depth)
        if v < 2:
            return gathered.at[0, pl.ds(first, count), half_of(v), rows, :]
        return gathered.at[chunk_of(v), pl.ds(first, count), :, rows, :]

    def part_span(v, p):
        count = tiles // parts_of(v)
        return p * count, count

    def same_place(v, first, count, index, ssem, rsem, target):
        return pltpu.make_async_remote_copy(
            src_ref=rows_of(v, first, count, index),
            dst_ref=rows_of(v, first, count, index),
            send_sem=ssem,
            recv_sem=rsem,
            device_id=(target, z),
            device_id_type=MESH,
        )

    def direct_copy(v, p, k, index):
        slot = slot_of(v, p)
        return same_place(
            v, *part_span(v, p), index, ag_ssem.at[slot, k], ag_rsem.at[slot, k], chip_at(direct[k]) * 2 + core
        )

    def relay_copy(v, p, k, index):
        slot = slot_of(v, p)
        first, count = part_span(v, p)
        return same_place(
            v,
            first + k * (count // 2),
            count // 2,
            index,
            rl_ssem.at[slot, k],
            rl_rsem.at[slot, k],
            chip_at(direct[1 - k]) * 2 + core,
        )

    def forward_copy(v, p, k, index):
        slot = slot_of(v, p)
        return same_place(v, *part_span(v, p), index, fw_ssem.at[slot, k], fw_rsem.at[slot, k], partner)

    def block_of(k, of_core):
        offset = 0 if k == 0 else direct[k - 1] if k <= len(direct) else 3
        return chip_at(offset) * 2 + of_core

    n_block = len(direct) + 1 + (1 if relayed else 0)

    def ag_start(v):
        for p in range(parts_of(v)):
            for k in range(len(direct)):
                direct_copy(v, p, k, me).start()
        for p in range(parts_of(v)):
            forward_copy(v, p, 0, me).start()

    def ag_relay(v, p):
        for k in range(len(direct)):
            index = block_of(k + 1, core)
            direct_copy(v, p, k, index).wait_recv()
            if relayed:
                relay_copy(v, p, k, index).start()
            forward_copy(v, p, k + 1, index).start()

    def ag_diag(v, p):
        if relayed:
            index = block_of(3, core)
            for k in range(2):
                relay_copy(v, p, k, index).wait_recv()
            forward_copy(v, p, 3, index).start()

    def ag_done(v, p):
        for k in range(n_block):
            forward_copy(v, p, k, block_of(k, 1 - core)).wait_recv()

    below, above = z, n_col - 1 - z
    skew = jnp.where(above > below, above - below, below - above)
    nearest = jnp.where(above > below, below, above)
    farthest = jnp.where(above > below, above, below)
    far_sign = jnp.where(above > below, 1, -1)

    def share_at(k):
        late = k - skew
        paired = z + (nearest - late // 2) * far_sign * (2 * (late % 2) - 1)
        return jnp.where(k < skew, z + far_sign * (farthest - k), paired)

    def partial_rows(v, item, share):
        rows = pl.ds(pl.multiple_of(share * quarter, quarter), quarter)
        members = [item] if v >= 2 else [item, item + half_held]
        lhs = jnp.concatenate([left_v[s, j, rows, :] for s in members for j in range(tiles)], axis=1)
        rhs = jnp.concatenate([coeffs[s].reshape(tiles * rank_width, width) for s in members], axis=0)
        return jnp.dot(lhs, rhs, preferred_element_type=jnp.float32)

    def piece_span(v, piece):
        first, count = items_of(v)
        if v < 2:
            return first + piece, 1, 0, quarter
        size = quarter // pieces_of(v)
        return first, count, piece * size, size

    def z_copy(v, share, piece, upward, target):
        c = chunk_of(v)
        item, count, row, size = piece_span(v, piece)
        return pltpu.make_async_remote_copy(
            src_ref=z_send.at[c, share, pl.ds(item, count), pl.ds(row, size), :],
            dst_ref=z_recv.at[upward, c, share, pl.ds(item, count), pl.ds(row, size), :],
            send_sem=z_ssem.at[v, share, piece],
            recv_sem=z_rsem.at[upward, v, share, piece],
            device_id=(me, target),
            device_id_type=MESH,
        )

    def flip(first, count):
        def tile(j, _):
            for s in range(held):
                for k in range(2):
                    rows = [
                        right_raw[s, j, d * depth + k * half_depth : d * depth + (k + 1) * half_depth, :]
                        for d in range(n_row)
                    ]
                    right_t[j, s * rank_width : (s + 1) * rank_width, k * half_block : (k + 1) * half_block] = (
                        jnp.concatenate(rows, axis=0).T
                    )
            return 0

        lax.fori_loop(first, first + count, tile, 0)

    def project(v, first, count):
        def tile(j, _):
            ids = lax.broadcasted_iota(jnp.int32, (rank_width, width), 0)
            if v < 2:
                packed = gathered[0, j, half_of(v)]
                turned = swapped(packed.astype(jnp.float32)).astype(jnp.bfloat16)
                split = half_held * rank_width
                lower = jnp.dot(
                    right_t[j, :split],
                    jnp.concatenate([packed, turned], axis=0),
                    preferred_element_type=jnp.float32,
                )
                upper = jnp.dot(
                    right_t[j, split:],
                    jnp.concatenate([turned, packed], axis=0),
                    preferred_element_type=jnp.float32,
                )
                for s in range(held):
                    low = s < half_held
                    at = s if low else s - half_held
                    part = (lower if low else upper)[at * rank_width : (at + 1) * rank_width]
                    lanes = low_lanes if low else jnp.logical_not(low_lanes)
                    keep = jnp.logical_and(ids < tile_ranks[s, j], lanes)
                    coeffs[s, j] = jnp.where(keep, part, 0.0).astype(jnp.bfloat16)
            else:
                products = jnp.dot(
                    right_t[j],
                    gathered[chunk_of(v), j].reshape(block, width),
                    preferred_element_type=jnp.float32,
                )
                for s in range(held):
                    part = products[s * rank_width : (s + 1) * rank_width]
                    coeffs[s, j] = jnp.where(ids < tile_ranks[s, j], part, 0.0).astype(jnp.bfloat16)
            return 0

        lax.fori_loop(first, first + count, tile, 0)

    def send_shares(v):
        c = chunk_of(v)
        base, n_item = items_of(v)

        def deliver(share, upward, target, has_input, piece):
            item, count, row, size = piece_span(v, piece)
            span = slice(row, row + size)

            @pl.when(has_input)
            def _():
                z_copy(v, share, piece, upward, target).wait_recv()
                for s in range(item, item + count):
                    total = share_part[s, span] + z_recv[upward, c, share, s, span].astype(jnp.float32)
                    z_send[c, share, s, span] = total.astype(jnp.bfloat16)

            @pl.when(jnp.logical_not(has_input))
            def _():
                for s in range(item, item + count):
                    z_send[c, share, s, span] = share_part[s, span].astype(jnp.bfloat16)

            z_copy(v, share, piece, upward, target).start()

        for k in range(n_col - 1):
            share = share_at(k)
            upward = jnp.where(share > z, 1, 0)
            target = z + 2 * upward - 1
            has_input = jnp.where(upward == 1, below, above) > 0
            if v < 2:
                for i in range(n_item):
                    share_part[base + i] = partial_rows(v, i, share)
                    deliver(share, upward, target, has_input, i)
            else:

                def row(s, _):
                    share_part[s] = partial_rows(v, s, share)
                    return 0

                lax.fori_loop(0, held, row, 0)
                for piece in range(pieces_of(v)):
                    deliver(share, upward, target, has_input, piece)

    def own_share(v):
        c = chunk_of(v)
        base, n_item = items_of(v)
        if v < 2:
            for i in range(n_item):
                own_part[c, base + i] = partial_rows(v, i, z)
        else:

            def row(s, _):
                own_part[c, s] = partial_rows(v, s, z)
                return 0

            lax.fori_loop(0, held, row, 0)

    def cuts_of(c):
        return LAST_PIECES if c == last else 1

    def exchange_copy(c, cut, d):
        size = quarter // cuts_of(c)
        span = pl.ds(cut * size, size)
        return pltpu.make_async_remote_copy(
            src_ref=a_send.at[c, d, span, :],
            dst_ref=a_recv[c + cut].at[d],
            send_sem=a_ssem.at[c + cut, d],
            recv_sem=a_rsem.at[c + cut, d],
            device_id=((me + d) % n_row, z),
            device_id_type=MESH,
        )

    def collect(v, pieces):
        c = chunk_of(v)
        for has_input, upward in ((below > 0, 1), (above > 0, 0)):

            @pl.when(has_input)
            def _():
                for piece in pieces:
                    item, count, row, size = piece_span(v, piece)
                    span = slice(row, row + size)
                    z_copy(v, z, piece, upward, z + 1 - 2 * upward).wait_recv()
                    for s in range(item, item + count):
                        own_part[c, s, span] = own_part[c, s, span] + z_recv[upward, c, z, s, span].astype(jnp.float32)

    def slots():
        found = []
        for d in range(n_row):
            target = (me + d) % n_row
            slot = jnp.int32(0)
            for s in range(held):
                slot = jnp.where(owner_map[me * held + s] // held == target, s, slot)
            found.append(slot)
        return found

    def finalize(c, cut, slot):
        size = quarter // cuts_of(c)
        span = slice(cut * size, (cut + 1) * size)
        if c == 0:
            for v in range(2):
                collect(v, range(pieces_of(v)))
            for i in range(half_held):
                one, two = own_part[0, i], own_part[0, half_held + i]
                final[i] = jnp.where(low_lanes, one, swapped(two)).astype(jnp.bfloat16)
                final[half_held + i] = jnp.where(low_lanes, swapped(one), two).astype(jnp.bfloat16)
        else:
            v = c + 1
            per = pieces_of(v) // cuts_of(c)
            collect(v, range(cut * per, (cut + 1) * per))
            for s in range(held):
                final[s, span] = own_part[c, s, span].astype(jnp.bfloat16)
        for d in range(n_row - 1, -1, -1):
            if d == 0:
                a_recv[c + cut][0] = final[slot[d], span]
            else:
                a_send[c, d, span] = final[slot[d], span]
                exchange_copy(c, cut, d).start()

    def shifts():
        found = []
        for k in range(held):
            wanted = me * held + k
            holder = jnp.int32(0)
            for s in range(n_row * held):
                holder = jnp.where(owner_map[s] == wanted, s // held, holder)
            found.append((me + n_row - holder) % n_row)
        return found

    def write_rows(c, cut, shift):
        size = quarter // cuts_of(c)
        span = slice(cut * size, (cut + 1) * size)
        for d in range(1, n_row):
            exchange_copy(c, cut, d).wait_recv()
        for k in range(held):
            out[k, span, c * width : (c + 1) * width] = a_recv[c + cut][shift[k]]

    def load_ready(v):
        if v >= 2:
            for k in range(2):
                own_load(chunk_of(v), k).wait()

    scope = jax.named_scope
    ag_start(0)
    with scope("rightwait"):
        right_load.wait()
    with scope("flip"):
        flip(0, tiles // 2)
    with scope("relay0"):
        for p in range(parts_of(0)):
            ag_relay(0, p)
        ag_start(1)
    with scope("flip2"):
        flip(tiles // 2, tiles // 2)
    slot, shift = slots(), shifts()
    with scope("diag0"):
        for p in range(parts_of(0)):
            ag_diag(0, p)
    for p in range(parts_of(0)):
        with scope(f"done0_{p}"):
            ag_done(0, p)
        with scope(f"proj0_{p}"):
            project(0, *part_span(0, p))
    left_load.wait()
    for v in range(n_step):
        if v > 0:
            for p in range(parts_of(v)):
                with scope(f"done{v}_{p}"):
                    ag_done(v, p)
                with scope(f"proj{v}_{p}"):
                    project(v, *part_span(v, p))
        with scope(f"relay{v+1}"):
            if v + 1 < n_step:
                for p in range(parts_of(v + 1)):
                    ag_relay(v + 1, p)
            if v + 2 < n_step:
                load_ready(v + 2)
                ag_start(v + 2)
        with scope(f"send{v}"):
            send_shares(v)
        with scope(f"diag{v+1}"):
            if v + 1 < n_step:
                for p in range(parts_of(v + 1)):
                    ag_diag(v + 1, p)
        with scope(f"own{v}"):
            own_share(v)
        if v >= 2:
            with scope(f"final{v-2}"):
                finalize(chunk_of(v) - 1, 0, slot)
        if v >= 3:
            with scope(f"write{v-3}"):
                write_rows(chunk_of(v) - 2, 0, shift)
    for cut in range(cuts_of(last)):
        with scope(f"finalL{cut}"):
            finalize(last, cut, slot)
    if last > 0:
        with scope(f"writeL"):
            write_rows(last - 1, 0, shift)
    for cut in range(cuts_of(last)):
        with scope(f"writeL{cut}"):
            write_rows(last, cut, shift)

    for v in range(n_step):
        for p in range(parts_of(v)):
            for k in range(len(direct)):
                direct_copy(v, p, k, me).wait_send()
                if relayed:
                    relay_copy(v, p, k, block_of(k + 1, core)).wait_send()
            for k in range(n_block):
                forward_copy(v, p, k, block_of(k, core)).wait_send()
        for k in range(n_col - 1):
            for piece in range(pieces_of(v)):
                z_copy(v, share_at(k), piece, 0, z).wait_send()
    for c in range(n_chunk):
        for cut in range(cuts_of(c)):
            for d in range(1, n_row):
                exchange_copy(c, cut, d).wait_send()


def on_device(n_row, n_col, vectors, right_factors, left_factors, tile_ranks, owner_map):
    held, tiles, block, rank_width = right_factors.shape
    width = LANES
    depth = vectors.shape[1]
    n_vec = vectors.shape[2]
    n_chunk = n_vec // width
    quarter = block // n_col
    direct, relayed = chip_steps(n_row // 2)
    n_slot = 2 * HALF_PARTS + (n_chunk - 1) * FULL_PARTS
    n_block = len(direct) + 1 + (1 if relayed else 0)
    n_piece = max(held // 2, MID_PIECES, LAST_PIECES)
    bf16, f32 = jnp.bfloat16, jnp.float32
    dma = pltpu.SemaphoreType.DMA
    smem = pl.BlockSpec(memory_space=pltpu.SMEM)
    hbm = pl.BlockSpec(memory_space=pl.ANY)
    return pl.pallas_call(
        functools.partial(kernel, n_row, n_col, n_chunk),
        out_shape=pltpu.VMEM((held, quarter, n_vec), bf16),
        in_specs=[smem, smem, hbm, hbm, hbm],
        out_specs=pl.BlockSpec(memory_space=pltpu.VMEM),
        scratch_shapes=[
            pltpu.VMEM((tiles, depth, width), bf16),
            pltpu.VMEM((n_chunk, tiles, 2, block // 2, width), bf16),
            pltpu.VMEM((held, tiles, block, rank_width), bf16),
            pltpu.VMEM((tiles, held * rank_width, block), bf16),
            pltpu.VMEM((held, tiles, block, rank_width), bf16),
            pltpu.VMEM((held, tiles, rank_width, width), bf16),
            pltpu.VMEM((held, quarter, width), f32),
            pltpu.VMEM((n_chunk, held, quarter, width), f32),
            pltpu.VMEM((n_chunk, n_col, held, quarter, width), bf16),
            pltpu.VMEM((2, n_chunk, n_col, held, quarter, width), bf16),
            pltpu.VMEM((held, quarter, width), bf16),
            pltpu.VMEM((n_chunk, n_row, quarter, width), bf16),
        ]
        + [pltpu.VMEM((n_row, quarter, width), bf16) for _ in range(n_chunk - 1)]
        + [pltpu.VMEM((n_row, quarter // LAST_PIECES, width), bf16) for _ in range(LAST_PIECES)]
        + [
            dma((2 * n_chunk,)),
            dma((2,)),
            dma((n_slot, len(direct))),
            dma((n_slot, len(direct))),
            dma((n_slot, 2)),
            dma((n_slot, 2)),
            dma((n_slot, n_block)),
            dma((n_slot, n_block)),
            dma((n_chunk + 1, n_col, n_piece)),
            dma((2, n_chunk + 1, n_col, n_piece)),
            dma((n_chunk + LAST_PIECES - 1, n_row)),
            dma((n_chunk + LAST_PIECES - 1, n_row)),
        ],
        compiler_params=pltpu.CompilerParams(
            collective_id=0, has_side_effects=True, vmem_limit_bytes=58000 * 1024
        ),
    )(owner_map, tile_ranks, vectors, right_factors, left_factors)


def solution(mesh):
    placed = (
        P("col", "row", None),
        P("row", "col", None, None),
        P("row", "col", None, None),
        P("row", "col"),
        P(),
    )
    body = functools.partial(on_device, mesh.shape["row"], mesh.shape["col"])
    return jax.shard_map(
        body, mesh=mesh, in_specs=placed, out_specs=P("row", "col", None), check_vma=False
    )
```

profile of v0, /device:TPU:8, one launch (start us, length us, event | category | flops | bytes accessed | tf_op | source)
XLA Modules:
  0.0 103.4 jit_solution(18190844063576834404)
XLA Ops:
  0.0 102.4 %shard_map.55 = bf16[4,256,512]{2,1,0:T(8,128)(2,1)S(1)} custom-call(s32[32]{0:T(128)} %owner_map.1, s32[4,8]{1,0:T(4,128)} %tile_ranks.1, bf16[8,128,512]{2,1,0:T(8,128)(2,1)} %vectors.1, bf16[4,8,1024,128]{3,2,1,0:T(8,128)(2,1)} %right.1, bf16[4,8,1024,128]{3,2,1,0:T(8,128)(2,1)} %left.1), custom_call_target="tpu_custom_call" | custom-call | tf_op jit(solution)/shard_map/pallas_call | solution.py:516
  102.4 1.0 copy.7
where the time goes:
time: 104 us; the launch traced here: 103 us
  Pallas kernels  102 us (98%)
    pallas_call x1, Pallas kernels, on_device(): pl.pallas_call(functools.partial(kernel, n_row, n_col, n_chunk), out_shap...  102 us

commit v1 on v0

--- a/solution.py
+++ b/solution.py
@@ -25,9 +25,7 @@
     a_send = scratch[11]
     n_land = n_chunk - 1 + LAST_PIECES
     a_recv = scratch[12 : 12 + n_land]
-    (load_sem, fac_sem, ag_ssem, ag_rsem, rl_ssem, rl_rsem, fw_ssem, fw_rsem, z_ssem, z_rsem, a_ssem, a_rsem) = scratch[
-        12 + n_land :
-    ]
+    (load_sem, fac_sem, send_sem, ag_rsem, rl_rsem, fw_rsem, z_rsem, a_rsem) = scratch[12 + n_land :]
     held, tiles, block, rank_width = right_raw.shape
     depth = vectors.shape[1]
     width = raw.shape[2]
@@ -93,7 +91,7 @@
         return pltpu.make_async_copy(
             vectors.at[:, pl.ds(k * half_depth, half_depth), pl.ds(c * width, width)],
             gathered.at[c, :, k, pl.ds(pl.multiple_of(me * half_depth, half_depth), half_depth), :],
-            load_sem.at[2 * c + k],
+            load_sem.at[1],
         )
 
     for c in range(1, n_chunk):
@@ -141,7 +139,7 @@
     def direct_copy(v, p, k, index):
         slot = slot_of(v, p)
         return same_place(
-            v, *part_span(v, p), index, ag_ssem.at[slot, k], ag_rsem.at[slot, k], chip_at(direct[k]) * 2 + core
+            v, *part_span(v, p), index, send_sem.at[0], ag_rsem.at[slot], chip_at(direct[k]) * 2 + core
         )
 
     def relay_copy(v, p, k, index):
@@ -152,14 +150,14 @@
             first + k * (count // 2),
             count // 2,
             index,
-            rl_ssem.at[slot, k],
-            rl_rsem.at[slot, k],
+            send_sem.at[1],
+            rl_rsem.at[slot],
             chip_at(direct[1 - k]) * 2 + core,
         )
 
     def forward_copy(v, p, k, index):
         slot = slot_of(v, p)
-        return same_place(v, *part_span(v, p), index, fw_ssem.at[slot, k], fw_rsem.at[slot, k], partner)
+        return same_place(v, *part_span(v, p), index, send_sem.at[2], fw_rsem.at[slot], partner)
 
     def block_of(k, of_core):
         offset = 0 if k == 0 else direct[k - 1] if k <= len(direct) else 3
@@ -167,31 +165,35 @@
 
     n_block = len(direct) + 1 + (1 if relayed else 0)
 
-    def ag_start(v):
-        for p in range(parts_of(v)):
-            for k in range(len(direct)):
-                direct_copy(v, p, k, me).start()
-        for p in range(parts_of(v)):
-            forward_copy(v, p, 0, me).start()
+    def blocks_wait(v, p, sem, blocks):
+        first, count = part_span(v, p)
+        rows = pl.ds(0, blocks * half_depth)
+        if v < 2:
+            ref = gathered.at[0, pl.ds(first, count), half_of(v), rows, :]
+        else:
+            ref = gathered.at[chunk_of(v), pl.ds(first, count), :, rows, :]
+        pltpu.make_async_copy(ref, ref, sem.at[slot_of(v, p)]).wait()
+
+    def ag_start(v, p):
+        for k in range(len(direct)):
+            direct_copy(v, p, k, me).start()
+        forward_copy(v, p, 0, me).start()
 
     def ag_relay(v, p):
+        blocks_wait(v, p, ag_rsem, len(direct))
         for k in range(len(direct)):
             index = block_of(k + 1, core)
-            direct_copy(v, p, k, index).wait_recv()
             if relayed:
                 relay_copy(v, p, k, index).start()
             forward_copy(v, p, k + 1, index).start()
 
     def ag_diag(v, p):
         if relayed:
-            index = block_of(3, core)
-            for k in range(2):
-                relay_copy(v, p, k, index).wait_recv()
-            forward_copy(v, p, 3, index).start()
+            blocks_wait(v, p, rl_rsem, 1)
+            forward_copy(v, p, 3, block_of(3, core)).start()
 
     def ag_done(v, p):
-        for k in range(n_block):
-            forward_copy(v, p, k, block_of(k, 1 - core)).wait_recv()
+        blocks_wait(v, p, fw_rsem, n_block)
 
     below, above = z, n_col - 1 - z
     skew = jnp.where(above > below, above - below, below - above)
@@ -218,14 +220,17 @@
         size = quarter // pieces_of(v)
         return first, count, piece * size, size
 
+    def first_piece(v):
+        return sum(pieces_of(u) for u in range(v))
+
     def z_copy(v, share, piece, upward, target):
         c = chunk_of(v)
         item, count, row, size = piece_span(v, piece)
         return pltpu.make_async_remote_copy(
             src_ref=z_send.at[c, share, pl.ds(item, count), pl.ds(row, size), :],
             dst_ref=z_recv.at[upward, c, share, pl.ds(item, count), pl.ds(row, size), :],
-            send_sem=z_ssem.at[v, share, piece],
-            recv_sem=z_rsem.at[upward, v, share, piece],
+            send_sem=send_sem.at[3],
+            recv_sem=z_rsem.at[first_piece(v) + piece, share + upward],
             device_id=(me, target),
             device_id_type=MESH,
         )
@@ -282,7 +287,7 @@
 
         lax.fori_loop(first, first + count, tile, 0)
 
-    def send_shares(v):
+    def send_shares(v, after):
         c = chunk_of(v)
         base, n_item = items_of(v)
 
@@ -322,6 +327,7 @@
                 lax.fori_loop(0, held, row, 0)
                 for piece in range(pieces_of(v)):
                     deliver(share, upward, target, has_input, piece)
+            after(k)
 
     def own_share(v):
         c = chunk_of(v)
@@ -346,8 +352,8 @@
         return pltpu.make_async_remote_copy(
             src_ref=a_send.at[c, d, span, :],
             dst_ref=a_recv[c + cut].at[d],
-            send_sem=a_ssem.at[c + cut, d],
-            recv_sem=a_rsem.at[c + cut, d],
+            send_sem=send_sem.at[4],
+            recv_sem=a_rsem.at[c + cut],
             device_id=((me + d) % n_row, z),
             device_id_type=MESH,
         )
@@ -411,18 +417,29 @@
     def write_rows(c, cut, shift):
         size = quarter // cuts_of(c)
         span = slice(cut * size, (cut + 1) * size)
-        for d in range(1, n_row):
-            exchange_copy(c, cut, d).wait_recv()
+        landed = a_recv[c + cut].at[pl.ds(1, n_row - 1)]
+        pltpu.make_async_copy(landed, landed, a_rsem.at[c + cut]).wait()
         for k in range(held):
             out[k, span, c * width : (c + 1) * width] = a_recv[c + cut][shift[k]]
 
-    def load_ready(v):
-        if v >= 2:
-            for k in range(2):
-                own_load(chunk_of(v), k).wait()
+    def load_ready():
+        if n_chunk > 1:
+            rest = gathered.at[pl.ds(1, last), :, :, pl.ds(0, half_depth), :]
+            pltpu.make_async_copy(rest, rest, load_sem.at[1]).wait()
 
     scope = jax.named_scope
-    ag_start(0)
+    inner = jnp.logical_and(below > 0, above > 0)
+
+    def drained(ref, k):
+        pltpu.make_async_copy(ref, ref, send_sem.at[k]).wait()
+
+    def start_all(v, parts=None):
+        for p in range(parts_of(v)) if parts is None else parts:
+            ag_start(v, p)
+
+    early = HALF_PARTS // 2
+    start_all(0)
+    start_all(1, range(early))
     with scope("rightwait"):
         right_load.wait()
     with scope("flip"):
@@ -430,19 +447,32 @@
     with scope("relay0"):
         for p in range(parts_of(0)):
             ag_relay(0, p)
-        ag_start(1)
+    start_all(1, range(early, HALF_PARTS))
     with scope("flip2"):
         flip(tiles // 2, tiles // 2)
     slot, shift = slots(), shifts()
+    left_load.wait()
+    load_ready()
     with scope("diag0"):
-        for p in range(parts_of(0)):
-            ag_diag(0, p)
+        ag_diag(0, 0)
     for p in range(parts_of(0)):
+        if p + 1 < parts_of(0):
+            with scope(f"diag0_{p+1}"):
+                ag_diag(0, p + 1)
         with scope(f"done0_{p}"):
             ag_done(0, p)
         with scope(f"proj0_{p}"):
             project(0, *part_span(0, p))
-    left_load.wait()
+        if p == 1:
+            with scope(f"relay1_a"):
+                for q in range(early):
+                    ag_relay(1, q)
+        if p == parts_of(0) - 2:
+            with scope(f"relay1_b"):
+                for q in range(early, HALF_PARTS):
+                    ag_relay(1, q)
+            if n_step > 2:
+                start_all(2)
     for v in range(n_step):
         if v > 0:
             for p in range(parts_of(v)):
@@ -450,52 +480,55 @@
                     ag_done(v, p)
                 with scope(f"proj{v}_{p}"):
                     project(v, *part_span(v, p))
-        with scope(f"relay{v+1}"):
-            if v + 1 < n_step:
-                for p in range(parts_of(v + 1)):
-                    ag_relay(v + 1, p)
+                if v + 1 < n_step and p + FULL_PARTS >= parts_of(v):
+                    with scope(f"relay{v+1}"):
+                        ag_relay(v + 1, p + FULL_PARTS - parts_of(v))
             if v + 2 < n_step:
-                load_ready(v + 2)
-                ag_start(v + 2)
+                start_all(v + 2)
+
+        def settle(v=v):
+            if v >= 2:
+                finalize(chunk_of(v) - 1, 0, slot)
+
+        def after(k, v=v):
+            @pl.when(inner)
+            def _():
+                if k == 0:
+                    own_share(v)
+                if k == min(1, n_col - 2):
+                    settle()
+
         with scope(f"send{v}"):
-            send_shares(v)
+            send_shares(v, after)
         with scope(f"diag{v+1}"):
             if v + 1 < n_step:
                 for p in range(parts_of(v + 1)):
                     ag_diag(v + 1, p)
         with scope(f"own{v}"):
-            own_share(v)
-        if v >= 2:
-            with scope(f"final{v-2}"):
-                finalize(chunk_of(v) - 1, 0, slot)
+
+            @pl.when(jnp.logical_not(inner))
+            def _():
+                own_share(v)
+                settle()
+
         if v >= 3:
             with scope(f"write{v-3}"):
                 write_rows(chunk_of(v) - 2, 0, shift)
+    drained(gathered.at[:, :, :, pl.ds(0, len(direct) * half_depth), :], 0)
+    if relayed:
+        drained(gathered.at[:, :, :, pl.ds(0, half_depth), :], 1)
+    drained(gathered.at[:, :, 0], 2)
     for cut in range(cuts_of(last)):
         with scope(f"finalL{cut}"):
             finalize(last, cut, slot)
+    drained(z_send.at[:, pl.ds(0, n_col - 1)], 3)
     if last > 0:
         with scope(f"writeL"):
             write_rows(last - 1, 0, shift)
     for cut in range(cuts_of(last)):
         with scope(f"writeL{cut}"):
             write_rows(last, cut, shift)
-
-    for v in range(n_step):
-        for p in range(parts_of(v)):
-            for k in range(len(direct)):
-                direct_copy(v, p, k, me).wait_send()
-                if relayed:
-                    relay_copy(v, p, k, block_of(k + 1, core)).wait_send()
-            for k in range(n_block):
-                forward_copy(v, p, k, block_of(k, core)).wait_send()
-        for k in range(n_col - 1):
-            for piece in range(pieces_of(v)):
-                z_copy(v, share_at(k), piece, 0, z).wait_send()
-    for c in range(n_chunk):
-        for cut in range(cuts_of(c)):
-            for d in range(1, n_row):
-                exchange_copy(c, cut, d).wait_send()
+    drained(a_send.at[:, pl.ds(1, n_row - 1)], 4)
 
 
 def on_device(n_row, n_col, vectors, right_factors, left_factors, tile_ranks, owner_map):
@@ -505,10 +538,8 @@
     n_vec = vectors.shape[2]
     n_chunk = n_vec // width
     quarter = block // n_col
-    direct, relayed = chip_steps(n_row // 2)
     n_slot = 2 * HALF_PARTS + (n_chunk - 1) * FULL_PARTS
-    n_block = len(direct) + 1 + (1 if relayed else 0)
-    n_piece = max(held // 2, MID_PIECES, LAST_PIECES)
+    n_piece = held + (n_chunk - 2) * MID_PIECES + LAST_PIECES
     bf16, f32 = jnp.bfloat16, jnp.float32
     dma = pltpu.SemaphoreType.DMA
     smem = pl.BlockSpec(memory_space=pltpu.SMEM)
@@ -535,18 +566,14 @@
         + [pltpu.VMEM((n_row, quarter, width), bf16) for _ in range(n_chunk - 1)]
         + [pltpu.VMEM((n_row, quarter // LAST_PIECES, width), bf16) for _ in range(LAST_PIECES)]
         + [
-            dma((2 * n_chunk,)),
             dma((2,)),
-            dma((n_slot, len(direct))),
-            dma((n_slot, len(direct))),
-            dma((n_slot, 2)),
-            dma((n_slot, 2)),
-            dma((n_slot, n_block)),
-            dma((n_slot, n_block)),
-            dma((n_chunk + 1, n_col, n_piece)),
-            dma((2, n_chunk + 1, n_col, n_piece)),
-            dma((n_chunk + LAST_PIECES - 1, n_row)),
-            dma((n_chunk + LAST_PIECES - 1, n_row)),
+            dma((2,)),
+            dma((5,)),
+            dma((n_slot,)),
+            dma((n_slot,)),
+            dma((n_slot,)),
+            dma((n_piece, n_col + 1)),
+            dma((n_chunk + LAST_PIECES - 1,)),
         ],
         compiler_params=pltpu.CompilerParams(
             collective_id=0, has_side_effects=True, vmem_limit_bytes=58000 * 1024

time: 104 us -> 94.6 us (0.910)
  Pallas kernels: 102 us -> 93.5 us
    pallas_call x1, Pallas kernels: 102 us -> 93.5 us  [on_device(): pl.pallas_call(functools.partial(kernel, n_row, n_col, n_chunk), out_shap...]
where the time goes in v1:
time: 94.6 us; the launch traced here: 94.4 us
  Pallas kernels  93.5 us (99%)
  local copies, waits for them, and re-layouts  0.97 us (1%)
    pallas_call x1, Pallas kernels, on_device(): pl.pallas_call(functools.partial(kernel, n_row, n_col, n_chunk), out_shap...  93.5 us

profile of v1, /device:TPU:8, one launch (start us, length us, event | category | flops | bytes accessed | tf_op | source)
XLA Modules:
  0.0 94.4 jit_solution(15289318306050192271)
XLA Ops:
  0.0 93.5 %shard_map.55 = bf16[4,256,512]{2,1,0:T(8,128)(2,1)S(1)} custom-call(s32[32]{0:T(128)} %owner_map.1, s32[4,8]{1,0:T(4,128)} %tile_ranks.1, bf16[8,128,512]{2,1,0:T(8,128)(2,1)} %vectors.1, bf16[4,8,1024,128]{3,2,1,0:T(8,128)(2,1)} %right.1, bf16[4,8,1024,128]{3,2,1,0:T(8,128)(2,1)} %left.1), custom_call_target="tpu_custom_call" | custom-call | tf_op jit(solution)/shard_map/pallas_call | solution.py:547
  93.5 1.0 %copy.7 = bf16[4,256,512]{2,1,0:T(8,128)(2,1)} copy(bf16[4,256,512]{2,1,0:T(8,128)(2,1)S(1)} %shard_map.55) | data formatting | bytes 2097152

commit v2 on v1

--- a/solution.py
+++ b/solution.py
@@ -13,11 +13,16 @@
 FULL_PARTS = 2
 MID_PIECES = 2
 LAST_PIECES = 4
+UNROLL = 2
 
 
 def chip_steps(n_chip):
     relayed = n_chip == 4
     return [1, 2] if relayed else list(range(1, n_chip)), relayed
+
+
+def edge_shares(n_col):
+    return sorted({1, max(n_col - 2, 0)})
 
 
 def kernel(n_row, n_col, n_chunk, owner_map, tile_ranks, vectors, right, left, out, *scratch):
@@ -25,7 +30,12 @@
     a_send = scratch[11]
     n_land = n_chunk - 1 + LAST_PIECES
     a_recv = scratch[12 : 12 + n_land]
-    (load_sem, fac_sem, send_sem, ag_rsem, rl_rsem, fw_rsem, z_rsem, a_rsem) = scratch[12 + n_land :]
+    p_send = scratch[12 + n_land]
+    early_shares = edge_shares(n_col)
+    p_recv = scratch[13 + n_land : 13 + n_land + len(early_shares)]
+    (load_sem, fac_sem, send_sem, ag_rsem, rl_rsem, fw_rsem, z_rsem, a_rsem, p_rsem) = scratch[
+        13 + n_land + len(early_shares) :
+    ]
     held, tiles, block, rank_width = right_raw.shape
     depth = vectors.shape[1]
     width = raw.shape[2]
@@ -105,7 +115,9 @@
 
     low_lanes = lax.broadcasted_iota(jnp.int32, (1, width), 1) < width // 2
 
-    first_load.wait()
+    scope = jax.named_scope
+    with scope('rawwait'):
+        first_load.wait()
     my_rows = pl.ds(pl.multiple_of(me * half_depth, half_depth), half_depth)
     for j in range(tiles):
         top = raw[j, :half_depth].astype(jnp.float32)
@@ -114,7 +126,8 @@
         gathered[0, j, 1, my_rows, :] = jnp.where(low_lanes, swapped(top), bottom).astype(jnp.bfloat16)
 
     both = jnp.where(z > 0, 1, 0) + jnp.where(z < n_col - 1, 1, 0)
-    pl.semaphore_wait(barrier, n_row - 1 + both)
+    with scope('barrier'):
+        pl.semaphore_wait(barrier, n_row - 1 + both)
 
     def rows_of(v, first, count, index):
         rows = pl.ds(pl.multiple_of(index * half_depth, half_depth), half_depth)
@@ -201,7 +214,11 @@
     farthest = jnp.where(above > below, above, below)
     far_sign = jnp.where(above > below, 1, -1)
 
-    def share_at(k):
+    def share_at(v, k):
+        if v < n_step - 1:
+            return jnp.where(
+                k < farthest, z + far_sign * (farthest - k), z - far_sign * (nearest + farthest - k)
+            )
         late = k - skew
         paired = z + (nearest - late // 2) * far_sign * (2 * (late % 2) - 1)
         return jnp.where(k < skew, z + far_sign * (farthest - k), paired)
@@ -210,7 +227,7 @@
         rows = pl.ds(pl.multiple_of(share * quarter, quarter), quarter)
         members = [item] if v >= 2 else [item, item + half_held]
         lhs = jnp.concatenate([left_v[s, j, rows, :] for s in members for j in range(tiles)], axis=1)
-        rhs = jnp.concatenate([coeffs[s].reshape(tiles * rank_width, width) for s in members], axis=0)
+        rhs = jnp.concatenate([coeffs[v % 2, s].reshape(tiles * rank_width, width) for s in members], axis=0)
         return jnp.dot(lhs, rhs, preferred_element_type=jnp.float32)
 
     def piece_span(v, piece):
@@ -273,7 +290,7 @@
                     part = (lower if low else upper)[at * rank_width : (at + 1) * rank_width]
                     lanes = low_lanes if low else jnp.logical_not(low_lanes)
                     keep = jnp.logical_and(ids < tile_ranks[s, j], lanes)
-                    coeffs[s, j] = jnp.where(keep, part, 0.0).astype(jnp.bfloat16)
+                    coeffs[v % 2, s, j] = jnp.where(keep, part, 0.0).astype(jnp.bfloat16)
             else:
                 products = jnp.dot(
                     right_t[j],
@@ -282,12 +299,12 @@
                 )
                 for s in range(held):
                     part = products[s * rank_width : (s + 1) * rank_width]
-                    coeffs[s, j] = jnp.where(ids < tile_ranks[s, j], part, 0.0).astype(jnp.bfloat16)
+                    coeffs[v % 2, s, j] = jnp.where(ids < tile_ranks[s, j], part, 0.0).astype(jnp.bfloat16)
             return 0
 
-        lax.fori_loop(first, first + count, tile, 0)
-
-    def send_shares(v, after):
+        lax.fori_loop(first, first + count, tile, 0, unroll=UNROLL)
+
+    def send_shares(v, before, after):
         c = chunk_of(v)
         base, n_item = items_of(v)
 
@@ -310,24 +327,105 @@
             z_copy(v, share, piece, upward, target).start()
 
         for k in range(n_col - 1):
-            share = share_at(k)
+            share = share_at(v, k)
             upward = jnp.where(share > z, 1, 0)
             target = z + 2 * upward - 1
             has_input = jnp.where(upward == 1, below, above) > 0
             if v < 2:
                 for i in range(n_item):
                     share_part[base + i] = partial_rows(v, i, share)
+                    if k == 0 and i == 0:
+                        before()
                     deliver(share, upward, target, has_input, i)
             else:
 
-                def row(s, _):
-                    share_part[s] = partial_rows(v, s, share)
-                    return 0
-
-                lax.fori_loop(0, held, row, 0)
+                def fill():
+                    def row(s, _):
+                        share_part[s] = partial_rows(v, s, share)
+                        return 0
+
+                    lax.fori_loop(0, held, row, 0)
+
+                if v == n_step - 1:
+
+                    @pl.when(jnp.logical_not(is_early(share)))
+                    def _():
+                        fill()
+
+                    for i, early in enumerate(early_shares):
+
+                        @pl.when(share == early)
+                        def _():
+                            early_wait(i)
+                            for k_row in range(held):
+                                share_part[k_row] = p_recv[i][shift[k_row]].astype(jnp.float32)
+                else:
+                    fill()
+                if k == 0:
+                    before()
                 for piece in range(pieces_of(v)):
                     deliver(share, upward, target, has_input, piece)
             after(k)
+
+    def is_early(share):
+        found = share == early_shares[0]
+        for early in early_shares[1:]:
+            found = jnp.logical_or(found, share == early)
+        return found
+
+    def early_copy(i, d):
+        return pltpu.make_async_remote_copy(
+            src_ref=p_send.at[i, d],
+            dst_ref=p_recv[i].at[d],
+            send_sem=send_sem.at[6],
+            recv_sem=p_rsem.at[i],
+            device_id=((me + d) % n_row, z),
+            device_id_type=MESH,
+        )
+
+    def early_start(i):
+        def row(s, _):
+            final[s] = partial_rows(n_step - 1, s, early_shares[i]).astype(jnp.bfloat16)
+            return 0
+
+        lax.fori_loop(0, held, row, 0)
+        for d in range(n_row - 1, -1, -1):
+            if d == 0:
+                p_recv[i][0] = final[slot[d]]
+            else:
+                p_send[i, d] = final[slot[d]]
+                early_copy(i, d).start()
+
+    def early_wait(i):
+        landed = p_recv[i].at[pl.ds(1, n_row - 1)]
+        pltpu.make_async_copy(landed, landed, p_rsem.at[i]).wait()
+
+    def own_last():
+        for i, early in enumerate(early_shares):
+
+            @pl.when(z == early)
+            def _():
+                early_wait(i)
+                for k in range(held):
+                    own_part[last, k] = p_recv[i][shift[k]].astype(jnp.float32)
+
+        @pl.when(jnp.logical_not(is_early(z)))
+        def _():
+            own_share(n_step - 1)
+
+    def finish(cut):
+        size = quarter // LAST_PIECES
+        span = slice(cut * size, (cut + 1) * size)
+
+        @pl.when(is_early(z))
+        def _():
+            collect(n_step - 1, [cut])
+            for k in range(held):
+                out[k, span, last * width :] = own_part[last, k, span].astype(jnp.bfloat16)
+
+        @pl.when(jnp.logical_not(is_early(z)))
+        def _():
+            finalize(last, cut, slot)
 
     def own_share(v):
         c = chunk_of(v)
@@ -352,7 +450,7 @@
         return pltpu.make_async_remote_copy(
             src_ref=a_send.at[c, d, span, :],
             dst_ref=a_recv[c + cut].at[d],
-            send_sem=send_sem.at[4],
+            send_sem=send_sem.at[5 if c == last else 4],
             recv_sem=a_rsem.at[c + cut],
             device_id=((me + d) % n_row, z),
             device_id_type=MESH,
@@ -427,7 +525,6 @@
             rest = gathered.at[pl.ds(1, last), :, :, pl.ds(0, half_depth), :]
             pltpu.make_async_copy(rest, rest, load_sem.at[1]).wait()
 
-    scope = jax.named_scope
     inner = jnp.logical_and(below > 0, above > 0)
 
     def drained(ref, k):
@@ -437,9 +534,7 @@
         for p in range(parts_of(v)) if parts is None else parts:
             ag_start(v, p)
 
-    early = HALF_PARTS // 2
     start_all(0)
-    start_all(1, range(early))
     with scope("rightwait"):
         right_load.wait()
     with scope("flip"):
@@ -447,69 +542,105 @@
     with scope("relay0"):
         for p in range(parts_of(0)):
             ag_relay(0, p)
-    start_all(1, range(early, HALF_PARTS))
+    start_all(1)
     with scope("flip2"):
         flip(tiles // 2, tiles // 2)
     slot, shift = slots(), shifts()
     left_load.wait()
     load_ready()
-    with scope("diag0"):
-        ag_diag(0, 0)
+    ahead = 3
+    for p in range(ahead):
+        with scope(f"diag0_{p}"):
+            ag_diag(0, p)
     for p in range(parts_of(0)):
-        if p + 1 < parts_of(0):
-            with scope(f"diag0_{p+1}"):
-                ag_diag(0, p + 1)
         with scope(f"done0_{p}"):
             ag_done(0, p)
         with scope(f"proj0_{p}"):
             project(0, *part_span(0, p))
-        if p == 1:
-            with scope(f"relay1_a"):
-                for q in range(early):
+        if p + ahead < parts_of(0):
+            with scope(f"diag0_{p+ahead}"):
+                ag_diag(0, p + ahead)
+        if p == parts_of(0) - 2:
+            with scope("relay1"):
+                for q in range(HALF_PARTS):
                     ag_relay(1, q)
-        if p == parts_of(0) - 2:
-            with scope(f"relay1_b"):
-                for q in range(early, HALF_PARTS):
-                    ag_relay(1, q)
-            if n_step > 2:
-                start_all(2)
+            start_all(2)
+    final_step = n_step - 1
     for v in range(n_step):
-        if v > 0:
+        if 0 < v < final_step:
             for p in range(parts_of(v)):
                 with scope(f"done{v}_{p}"):
                     ag_done(v, p)
                 with scope(f"proj{v}_{p}"):
                     project(v, *part_span(v, p))
-                if v + 1 < n_step and p + FULL_PARTS >= parts_of(v):
-                    with scope(f"relay{v+1}"):
-                        ag_relay(v + 1, p + FULL_PARTS - parts_of(v))
-            if v + 2 < n_step:
-                start_all(v + 2)
+                if p == parts_of(v) - 2 and v + 1 < final_step:
+                    with scope(f"relay{v+1}_0"):
+                        ag_relay(v + 1, 0)
+                    if v + 2 == final_step:
+                        start_all(final_step)
 
         def settle(v=v):
             if v >= 2:
                 finalize(chunk_of(v) - 1, 0, slot)
 
-        def after(k, v=v):
+        def before(v=v):
+            if 0 < v < final_step:
+                if v + 1 < final_step:
+                    with scope(f"relay{v+1}_1"):
+                        for p in range(1, parts_of(v + 1)):
+                            ag_relay(v + 1, p)
+                if v + 2 < final_step:
+                    start_all(v + 2)
+
             @pl.when(inner)
             def _():
-                if k == 0:
-                    own_share(v)
-                if k == min(1, n_col - 2):
+                if v < final_step:
+                    with scope(f"iown{v}"):
+                        own_share(v)
+                if v < final_step:
+                    with scope(f"isettle{v}"):
+                        settle()
+
+        def after(k, v=v):
+            if k == 0 and v == final_step:
+
+                @pl.when(inner)
+                def _():
                     settle()
 
+            if k == 0 and v == final_step - 1:
+                with scope("diagL"):
+                    for p in range(parts_of(final_step)):
+                        ag_diag(final_step, p)
+                for p in range(parts_of(final_step)):
+                    with scope("doneL"):
+                        ag_done(final_step, p)
+                    with scope("projL"):
+                        project(final_step, *part_span(final_step, p))
+                with scope("early"):
+                    for i in range(len(early_shares)):
+                        early_start(i)
+
         with scope(f"send{v}"):
-            send_shares(v, after)
-        with scope(f"diag{v+1}"):
-            if v + 1 < n_step:
+            send_shares(v, before, after)
+        if v + 1 < final_step:
+            with scope(f"diag{v+1}"):
                 for p in range(parts_of(v + 1)):
                     ag_diag(v + 1, p)
+        if v == final_step - 2:
+            with scope("relayL"):
+                for p in range(parts_of(final_step)):
+                    ag_relay(final_step, p)
         with scope(f"own{v}"):
 
             @pl.when(jnp.logical_not(inner))
             def _():
-                own_share(v)
+                if v < final_step:
+                    own_share(v)
                 settle()
+
+        if v == final_step:
+            own_last()
 
         if v >= 3:
             with scope(f"write{v-3}"):
@@ -518,17 +649,26 @@
     if relayed:
         drained(gathered.at[:, :, :, pl.ds(0, half_depth), :], 1)
     drained(gathered.at[:, :, 0], 2)
+    drained(a_send.at[pl.ds(0, last), pl.ds(1, n_row - 1)], 4)
+    drained(p_send.at[:, pl.ds(1, n_row - 1)], 6)
+
+    def write_before():
+        with scope("writeL"):
+            write_rows(last - 1, 0, shift)
+
+    pl.when(is_early(z))(write_before)
     for cut in range(cuts_of(last)):
         with scope(f"finalL{cut}"):
-            finalize(last, cut, slot)
+            finish(cut)
+    pl.when(jnp.logical_not(is_early(z)))(write_before)
     drained(z_send.at[:, pl.ds(0, n_col - 1)], 3)
-    if last > 0:
-        with scope(f"writeL"):
-            write_rows(last - 1, 0, shift)
-    for cut in range(cuts_of(last)):
-        with scope(f"writeL{cut}"):
-            write_rows(last, cut, shift)
-    drained(a_send.at[:, pl.ds(1, n_row - 1)], 4)
+
+    @pl.when(jnp.logical_not(is_early(z)))
+    def _():
+        for cut in range(cuts_of(last)):
+            with scope(f"writeL{cut}"):
+                write_rows(last, cut, shift)
+        drained(a_send.at[last, pl.ds(1, n_row - 1)], 5)
 
 
 def on_device(n_row, n_col, vectors, right_factors, left_factors, tile_ranks, owner_map):
@@ -539,6 +679,7 @@
     n_chunk = n_vec // width
     quarter = block // n_col
     n_slot = 2 * HALF_PARTS + (n_chunk - 1) * FULL_PARTS
+    n_early = len(edge_shares(n_col))
     n_piece = held + (n_chunk - 2) * MID_PIECES + LAST_PIECES
     bf16, f32 = jnp.bfloat16, jnp.float32
     dma = pltpu.SemaphoreType.DMA
@@ -555,7 +696,7 @@
             pltpu.VMEM((held, tiles, block, rank_width), bf16),
             pltpu.VMEM((tiles, held * rank_width, block), bf16),
             pltpu.VMEM((held, tiles, block, rank_width), bf16),
-            pltpu.VMEM((held, tiles, rank_width, width), bf16),
+            pltpu.VMEM((2, held, tiles, rank_width, width), bf16),
             pltpu.VMEM((held, quarter, width), f32),
             pltpu.VMEM((n_chunk, held, quarter, width), f32),
             pltpu.VMEM((n_chunk, n_col, held, quarter, width), bf16),
@@ -565,15 +706,18 @@
         ]
         + [pltpu.VMEM((n_row, quarter, width), bf16) for _ in range(n_chunk - 1)]
         + [pltpu.VMEM((n_row, quarter // LAST_PIECES, width), bf16) for _ in range(LAST_PIECES)]
+        + [pltpu.VMEM((n_early, n_row, quarter, width), bf16)]
+        + [pltpu.VMEM((n_row, quarter, width), bf16) for _ in range(n_early)]
         + [
             dma((2,)),
             dma((2,)),
-            dma((5,)),
+            dma((7,)),
             dma((n_slot,)),
             dma((n_slot,)),
             dma((n_slot,)),
             dma((n_piece, n_col + 1)),
             dma((n_chunk + LAST_PIECES - 1,)),
+            dma((n_early,)),
         ],
         compiler_params=pltpu.CompilerParams(
             collective_id=0, has_side_effects=True, vmem_limit_bytes=58000 * 1024

time: 94.6 us -> 89.8 us (0.949)
  the two profiles are of different devices: /device:TPU:8 before, /device:TPU:0 now
where the time goes in v2:
time: 89.8 us; the launch traced here: 89.6 us
  Pallas kernels  88.6 us (99%)
  local copies, waits for them, and re-layouts  0.97 us (1%)
    pallas_call x1, Pallas kernels, on_device(): pl.pallas_call(functools.partial(kernel, n_row, n_col, n_chunk), out_shap...  88.6 us

profile of v2, /device:TPU:0, one launch (start us, length us, event | category | flops | bytes accessed | tf_op | source)
XLA Modules:
  0.0 89.6 jit_solution(16179250330169256430)
XLA Ops:
  0.0 88.6 %shard_map.55 = bf16[4,256,512]{2,1,0:T(8,128)(2,1)S(1)} custom-call(s32[32]{0:T(128)} %owner_map.1, s32[4,8]{1,0:T(4,128)} %tile_ranks.1, bf16[8,128,512]{2,1,0:T(8,128)(2,1)} %vectors.1, bf16[4,8,1024,128]{3,2,1,0:T(8,128)(2,1)} %right.1, bf16[4,8,1024,128]{3,2,1,0:T(8,128)(2,1)} %left.1), custom_call_target="tpu_custom_call" | custom-call | tf_op jit(solution)/shard_map/pallas_call | solution.py:688
  88.6 1.0 %copy.7 = bf16[4,256,512]{2,1,0:T(8,128)(2,1)} copy(bf16[4,256,512]{2,1,0:T(8,128)(2,1)S(1)} %shard_map.55) | data formatting | bytes 2097152

commit v3 on v2

--- a/solution.py
+++ b/solution.py
@@ -21,6 +21,10 @@
     return [1, 2] if relayed else list(range(1, n_chip)), relayed
 
 
+def cuts_in(n_chunk, c):
+    return LAST_PIECES if c == n_chunk - 1 else MID_PIECES if 0 < c == n_chunk - 2 else 1
+
+
 def edge_shares(n_col):
     return sorted({1, max(n_col - 2, 0)})
 
@@ -28,7 +32,7 @@
 def kernel(n_row, n_col, n_chunk, owner_map, tile_ranks, vectors, right, left, out, *scratch):
     (raw, gathered, right_raw, right_t, left_v, coeffs, share_part, own_part, z_send, z_recv, final) = scratch[:11]
     a_send = scratch[11]
-    n_land = n_chunk - 1 + LAST_PIECES
+    n_land = sum(cuts_in(n_chunk, c) for c in range(n_chunk))
     a_recv = scratch[12 : 12 + n_land]
     p_send = scratch[12 + n_land]
     early_shares = edge_shares(n_col)
@@ -209,13 +213,14 @@
         blocks_wait(v, p, fw_rsem, n_block)
 
     below, above = z, n_col - 1 - z
+    inner = jnp.logical_and(below > 0, above > 0)
     skew = jnp.where(above > below, above - below, below - above)
     nearest = jnp.where(above > below, below, above)
     farthest = jnp.where(above > below, above, below)
     far_sign = jnp.where(above > below, 1, -1)
 
     def share_at(v, k):
-        if v < n_step - 1:
+        if v < n_step - 2:
             return jnp.where(
                 k < farthest, z + far_sign * (farthest - k), z - far_sign * (nearest + farthest - k)
             )
@@ -308,7 +313,7 @@
         c = chunk_of(v)
         base, n_item = items_of(v)
 
-        def deliver(share, upward, target, has_input, piece):
+        def deliver(k, share, upward, target, has_input, piece):
             item, count, row, size = piece_span(v, piece)
             span = slice(row, row + size)
 
@@ -316,15 +321,38 @@
             def _():
                 z_copy(v, share, piece, upward, target).wait_recv()
                 for s in range(item, item + count):
-                    total = share_part[s, span] + z_recv[upward, c, share, s, span].astype(jnp.float32)
+                    total = share_part[k % 2, s, span] + z_recv[upward, c, share, s, span].astype(jnp.float32)
                     z_send[c, share, s, span] = total.astype(jnp.bfloat16)
 
             @pl.when(jnp.logical_not(has_input))
             def _():
                 for s in range(item, item + count):
-                    z_send[c, share, s, span] = share_part[s, span].astype(jnp.bfloat16)
+                    z_send[c, share, s, span] = share_part[k % 2, s, span].astype(jnp.bfloat16)
 
             z_copy(v, share, piece, upward, target).start()
+
+        def fill(k):
+            share = share_at(v, k)
+
+            def row(s, _):
+                share_part[k % 2, s] = partial_rows(v, s, share)
+                return 0
+
+            if v < n_step - 1:
+                lax.fori_loop(0, held, row, 0)
+                return
+
+            @pl.when(jnp.logical_not(is_early(share)))
+            def _():
+                lax.fori_loop(0, held, row, 0)
+
+            for i, early in enumerate(early_shares):
+
+                @pl.when(share == early)
+                def _():
+                    early_wait(i)
+                    for at in range(held):
+                        share_part[k % 2, at] = p_recv[i][shift[at]].astype(jnp.float32)
 
         for k in range(n_col - 1):
             share = share_at(v, k)
@@ -333,38 +361,21 @@
             has_input = jnp.where(upward == 1, below, above) > 0
             if v < 2:
                 for i in range(n_item):
-                    share_part[base + i] = partial_rows(v, i, share)
+                    share_part[k % 2, base + i] = partial_rows(v, i, share)
                     if k == 0 and i == 0:
                         before()
-                    deliver(share, upward, target, has_input, i)
+                    deliver(k, share, upward, target, has_input, i)
             else:
-
-                def fill():
-                    def row(s, _):
-                        share_part[s] = partial_rows(v, s, share)
-                        return 0
-
-                    lax.fori_loop(0, held, row, 0)
-
-                if v == n_step - 1:
-
-                    @pl.when(jnp.logical_not(is_early(share)))
-                    def _():
-                        fill()
-
-                    for i, early in enumerate(early_shares):
-
-                        @pl.when(share == early)
-                        def _():
-                            early_wait(i)
-                            for k_row in range(held):
-                                share_part[k_row] = p_recv[i][shift[k_row]].astype(jnp.float32)
+                if v == n_step - 1 and k == 1:
+                    pl.when(jnp.logical_not(inner))(functools.partial(fill, k))
                 else:
-                    fill()
+                    fill(k)
                 if k == 0:
                     before()
+                    if v == n_step - 1 and n_col > 2:
+                        pl.when(inner)(functools.partial(fill, 1))
                 for piece in range(pieces_of(v)):
-                    deliver(share, upward, target, has_input, piece)
+                    deliver(k, share, upward, target, has_input, piece)
             after(k)
 
     def is_early(share):
@@ -441,17 +452,17 @@
 
             lax.fori_loop(0, held, row, 0)
 
-    def cuts_of(c):
-        return LAST_PIECES if c == last else 1
+    def land_at(c, cut):
+        return sum(cuts_in(n_chunk, u) for u in range(c)) + cut
 
     def exchange_copy(c, cut, d):
-        size = quarter // cuts_of(c)
+        size = quarter // cuts_in(n_chunk, c)
         span = pl.ds(cut * size, size)
         return pltpu.make_async_remote_copy(
             src_ref=a_send.at[c, d, span, :],
-            dst_ref=a_recv[c + cut].at[d],
+            dst_ref=a_recv[land_at(c, cut)].at[d],
             send_sem=send_sem.at[5 if c == last else 4],
-            recv_sem=a_rsem.at[c + cut],
+            recv_sem=a_rsem.at[land_at(c, cut)],
             device_id=((me + d) % n_row, z),
             device_id_type=MESH,
         )
@@ -480,7 +491,7 @@
         return found
 
     def finalize(c, cut, slot):
-        size = quarter // cuts_of(c)
+        size = quarter // cuts_in(n_chunk, c)
         span = slice(cut * size, (cut + 1) * size)
         if c == 0:
             for v in range(2):
@@ -491,13 +502,13 @@
                 final[half_held + i] = jnp.where(low_lanes, swapped(one), two).astype(jnp.bfloat16)
         else:
             v = c + 1
-            per = pieces_of(v) // cuts_of(c)
+            per = pieces_of(v) // cuts_in(n_chunk, c)
             collect(v, range(cut * per, (cut + 1) * per))
             for s in range(held):
                 final[s, span] = own_part[c, s, span].astype(jnp.bfloat16)
         for d in range(n_row - 1, -1, -1):
             if d == 0:
-                a_recv[c + cut][0] = final[slot[d], span]
+                a_recv[land_at(c, cut)][0] = final[slot[d], span]
             else:
                 a_send[c, d, span] = final[slot[d], span]
                 exchange_copy(c, cut, d).start()
@@ -513,19 +524,18 @@
         return found
 
     def write_rows(c, cut, shift):
-        size = quarter // cuts_of(c)
+        size = quarter // cuts_in(n_chunk, c)
         span = slice(cut * size, (cut + 1) * size)
-        landed = a_recv[c + cut].at[pl.ds(1, n_row - 1)]
-        pltpu.make_async_copy(landed, landed, a_rsem.at[c + cut]).wait()
+        landed = a_recv[land_at(c, cut)].at[pl.ds(1, n_row - 1)]
+        pltpu.make_async_copy(landed, landed, a_rsem.at[land_at(c, cut)]).wait()
         for k in range(held):
-            out[k, span, c * width : (c + 1) * width] = a_recv[c + cut][shift[k]]
+            out[k, span, c * width : (c + 1) * width] = a_recv[land_at(c, cut)][shift[k]]
 
     def load_ready():
         if n_chunk > 1:
             rest = gathered.at[pl.ds(1, last), :, :, pl.ds(0, half_depth), :]
             pltpu.make_async_copy(rest, rest, load_sem.at[1]).wait()
 
-    inner = jnp.logical_and(below > 0, above > 0)
 
     def drained(ref, k):
         pltpu.make_async_copy(ref, ref, send_sem.at[k]).wait()
@@ -548,7 +558,7 @@
     slot, shift = slots(), shifts()
     left_load.wait()
     load_ready()
-    ahead = 3
+    ahead = 2
     for p in range(ahead):
         with scope(f"diag0_{p}"):
             ag_diag(0, p)
@@ -560,9 +570,13 @@
         if p + ahead < parts_of(0):
             with scope(f"diag0_{p+ahead}"):
                 ag_diag(0, p + ahead)
-        if p == parts_of(0) - 2:
+        if p == 1:
             with scope("relay1"):
-                for q in range(HALF_PARTS):
+                for q in range(HALF_PARTS // 2):
+                    ag_relay(1, q)
+        if p == 2:
+            with scope("relay1"):
+                for q in range(HALF_PARTS // 2, HALF_PARTS):
                     ag_relay(1, q)
             start_all(2)
     final_step = n_step - 1
@@ -581,7 +595,8 @@
 
         def settle(v=v):
             if v >= 2:
-                finalize(chunk_of(v) - 1, 0, slot)
+                for cut in range(cuts_in(n_chunk, chunk_of(v) - 1)):
+                    finalize(chunk_of(v) - 1, cut, slot)
 
         def before(v=v):
             if 0 < v < final_step:
@@ -591,10 +606,14 @@
                             ag_relay(v + 1, p)
                 if v + 2 < final_step:
                     start_all(v + 2)
+            if v == final_step - 1:
+                with scope("diagL"):
+                    for p in range(parts_of(final_step)):
+                        ag_diag(final_step, p)
 
             @pl.when(inner)
             def _():
-                if v < final_step:
+                if v < final_step - 1:
                     with scope(f"iown{v}"):
                         own_share(v)
                 if v < final_step:
@@ -602,16 +621,10 @@
                         settle()
 
         def after(k, v=v):
-            if k == 0 and v == final_step:
-
-                @pl.when(inner)
-                def _():
-                    settle()
+            if k == min(1, n_col - 2) and v == final_step:
+                pl.when(inner)(settle)
 
             if k == 0 and v == final_step - 1:
-                with scope("diagL"):
-                    for p in range(parts_of(final_step)):
-                        ag_diag(final_step, p)
                 for p in range(parts_of(final_step)):
                     with scope("doneL"):
                         ag_done(final_step, p)
@@ -631,6 +644,8 @@
             with scope("relayL"):
                 for p in range(parts_of(final_step)):
                     ag_relay(final_step, p)
+        if v == final_step - 1:
+            pl.when(inner)(functools.partial(own_share, v))
         with scope(f"own{v}"):
 
             @pl.when(jnp.logical_not(inner))
@@ -649,23 +664,24 @@
     if relayed:
         drained(gathered.at[:, :, :, pl.ds(0, half_depth), :], 1)
     drained(gathered.at[:, :, 0], 2)
-    drained(a_send.at[pl.ds(0, last), pl.ds(1, n_row - 1)], 4)
-    drained(p_send.at[:, pl.ds(1, n_row - 1)], 6)
 
     def write_before():
         with scope("writeL"):
-            write_rows(last - 1, 0, shift)
+            for cut in range(cuts_in(n_chunk, last - 1)):
+                write_rows(last - 1, cut, shift)
 
     pl.when(is_early(z))(write_before)
-    for cut in range(cuts_of(last)):
+    for cut in range(cuts_in(n_chunk, last)):
         with scope(f"finalL{cut}"):
             finish(cut)
     pl.when(jnp.logical_not(is_early(z)))(write_before)
+    drained(a_send.at[pl.ds(0, last), pl.ds(1, n_row - 1)], 4)
+    drained(p_send.at[:, pl.ds(1, n_row - 1)], 6)
     drained(z_send.at[:, pl.ds(0, n_col - 1)], 3)
 
     @pl.when(jnp.logical_not(is_early(z)))
     def _():
-        for cut in range(cuts_of(last)):
+        for cut in range(cuts_in(n_chunk, last)):
             with scope(f"writeL{cut}"):
                 write_rows(last, cut, shift)
         drained(a_send.at[last, pl.ds(1, n_row - 1)], 5)
@@ -680,6 +696,7 @@
     quarter = block // n_col
     n_slot = 2 * HALF_PARTS + (n_chunk - 1) * FULL_PARTS
     n_early = len(edge_shares(n_col))
+    land_cuts = [cuts_in(n_chunk, c) for c in range(n_chunk) for _ in range(cuts_in(n_chunk, c))]
     n_piece = held + (n_chunk - 2) * MID_PIECES + LAST_PIECES
     bf16, f32 = jnp.bfloat16, jnp.float32
     dma = pltpu.SemaphoreType.DMA
@@ -697,15 +714,14 @@
             pltpu.VMEM((tiles, held * rank_width, block), bf16),
             pltpu.VMEM((held, tiles, block, rank_width), bf16),
             pltpu.VMEM((2, held, tiles, rank_width, width), bf16),
-            pltpu.VMEM((held, quarter, width), f32),
+            pltpu.VMEM((2, held, quarter, width), f32),
             pltpu.VMEM((n_chunk, held, quarter, width), f32),
             pltpu.VMEM((n_chunk, n_col, held, quarter, width), bf16),
             pltpu.VMEM((2, n_chunk, n_col, held, quarter, width), bf16),
             pltpu.VMEM((held, quarter, width), bf16),
             pltpu.VMEM((n_chunk, n_row, quarter, width), bf16),
         ]
-        + [pltpu.VMEM((n_row, quarter, width), bf16) for _ in range(n_chunk - 1)]
-        + [pltpu.VMEM((n_row, quarter // LAST_PIECES, width), bf16) for _ in range(LAST_PIECES)]
+        + [pltpu.VMEM((n_row, quarter // cuts, width), bf16) for cuts in land_cuts]
         + [pltpu.VMEM((n_early, n_row, quarter, width), bf16)]
         + [pltpu.VMEM((n_row, quarter, width), bf16) for _ in range(n_early)]
         + [
@@ -716,7 +732,7 @@
             dma((n_slot,)),
             dma((n_slot,)),
             dma((n_piece, n_col + 1)),
-            dma((n_chunk + LAST_PIECES - 1,)),
+            dma((len(land_cuts),)),
             dma((n_early,)),
         ],
         compiler_params=pltpu.CompilerParams(

time: 89.8 us -> 88.5 us (0.986)
  Pallas kernels: 88.6 us -> 87.3 us
    pallas_call x1, Pallas kernels: 88.6 us -> 87.3 us  [on_device(): pl.pallas_call(functools.partial(kernel, n_row, n_col, n_chunk), out_shap...]
where the time goes in v3:
time: 88.5 us; the launch traced here: 88.3 us
  Pallas kernels  87.3 us (99%)
  local copies, waits for them, and re-layouts  0.97 us (1%)
    pallas_call x1, Pallas kernels, on_device(): pl.pallas_call(functools.partial(kernel, n_row, n_col, n_chunk), out_shap...  87.3 us

profile of v3, /device:TPU:0, one launch (start us, length us, event | category | flops | bytes accessed | tf_op | source)
XLA Modules:
  0.0 88.3 jit_solution(2257029228561444219)
XLA Ops:
  0.0 87.3 %shard_map.55 = bf16[4,256,512]{2,1,0:T(8,128)(2,1)S(1)} custom-call(s32[32]{0:T(128)} %owner_map.1, s32[4,8]{1,0:T(4,128)} %tile_ranks.1, bf16[8,128,512]{2,1,0:T(8,128)(2,1)} %vectors.1, bf16[4,8,1024,128]{3,2,1,0:T(8,128)(2,1)} %right.1, bf16[4,8,1024,128]{3,2,1,0:T(8,128)(2,1)} %left.1), custom_call_target="tpu_custom_call" | custom-call | tf_op jit(solution)/shard_map/pallas_call | solution.py:705
  87.4 1.0 %copy.7 = bf16[4,256,512]{2,1,0:T(8,128)(2,1)} copy(bf16[4,256,512]{2,1,0:T(8,128)(2,1)S(1)} %shard_map.55) | data formatting | bytes 2097152
